TPU v7x, 32 devices: a whole 2x2x4 slice. The times are simulated.
32 devices in a mesh: expert: 8 (over z, y), vocab: 4 (over x, core).
Axes of the slice: x: 2, y: 2, z: 4, core: 2. Of those that a mesh axis runs over, the one named last changes fastest.
Arguments:
- layer_out: bfloat16 [256, 2048], P('expert'), may hold values from -6 to 6
- moe_input: bfloat16 [256, 2048], P('expert'), may hold values from -6 to 6
- final_gain: float32 [2048], replicated, may hold values from 0.1 to 1.9
- head_weight: bfloat16 [2048, 12288], P(None, ('expert', 'vocab')), may hold values from -0.125 to 0.125
- clean_ids: int32 [256], P('expert'), may hold values from 0 to 12287
- levels: int32 [256], P('expert'), may hold values from 0 to 15
- ratio_table: float32 [16], replicated, may hold values from 0.5 to 8
- gate_weights: float32 [256, 8], P('expert'), may hold values from 0.05 to 0.5
- expert_ids: int32 [256, 8], P('expert'), may hold values from 0 to 15, all different within a row; in each aligned block of 32 rows (0 to 31, 32 to 63, ...) at most 32 rows name the same one
- w_gate: bfloat16 [16, 2048, 1024], P('expert', None, 'vocab'), may hold values from -0.125 to 0.125
- w_up: bfloat16 [16, 2048, 1024], P('expert', None, 'vocab'), may hold values from -0.125 to 0.125
- w_down: bfloat16 [16, 1024, 2048], P('expert', 'vocab'), may hold values from -0.1875 to 0.1875
Outputs:
- head_grad: float32 [2048, 12288], P(None, ('expert', 'vocab'))
- residual_grad: float32 [256, 2048], P('expert', 'vocab')
- input_grad: float32 [256, 2048], P('expert', 'vocab')
Inputs may be any that keep to these rules, and one draw needn't show every extreme that they name: `expert_ids`: the 8 experts of a row are distinct; among the 32 rows of one index of expert no expert is named by more than 32 rows.
All inputs are finite; a program needn't handle non-finite values.
Results may differ from a plain program's by a relative error of at most 0.0044.
The roundings to bfloat16 on the way count: a program that leaves them out, or rounds other values in their place, can miss the bound.
Values may be sent and summed in bfloat16 or wider, within the bound.
A program may use at most 64 MiB of HBM per device.

v0:
```python
import math

import jax
import jax.numpy as jnp
from jax import lax
from jax.sharding import PartitionSpec as P

epsilon = 1e-05


def on_device(
    layer_out,
    moe_input,
    final_gain,
    head_weight,
    clean_ids,
    levels,
    ratio_table,
    gate_weights,
    expert_ids,
    w_gate,
    w_up,
    w_down,
):
    rows_local, model_width = layer_out.shape
    top_count = expert_ids.shape[1]
    n_expert = lax.axis_size("expert")
    n_vocab = lax.axis_size("vocab")
    total_rows = rows_local * n_expert
    local_experts = w_gate.shape[0]
    experts_all = local_experts * n_expert
    capacity = max(2, 2 * rows_local * top_count // experts_all)
    feature_share = model_width // n_vocab
    vocab_local = head_weight.shape[1]
    values = layer_out.astype(jnp.float32)
    row_scale = jnp.sqrt(jnp.mean(values * values, axis=1, keepdims=True) + epsilon)
    unit_rows = values / row_scale
    normed = (unit_rows * final_gain[None, :]).astype(jnp.bfloat16)
    normed_all, clean_all, level_all = (
        lax.all_gather(normed, "expert", axis=0, tiled=True),
        lax.all_gather(clean_ids, "expert", axis=0, tiled=True),
        lax.all_gather(levels, "expert", axis=0, tiled=True),
    )
    level_labels = jnp.arange(ratio_table.shape[0], dtype=jnp.int32)
    ratio_rows = jnp.sum(
        jnp.where(level_all[:, None] == level_labels[None, :], ratio_table[None, :], 0.0), axis=1
    )
    column_start = (lax.axis_index("expert") * n_vocab + lax.axis_index("vocab")) * vocab_local
    columns = column_start + jnp.arange(vocab_local, dtype=jnp.int32)
    scores = jnp.dot(normed_all, head_weight, preferred_element_type=jnp.float32)
    target_hit = (clean_all[:, None] == columns[None, :]).astype(jnp.float32)
    loss_scale = 1.0 / math.sqrt(total_rows)
    score_grad = ((jnp.exp(scores) - ratio_rows[:, None] * target_hit) * loss_scale).astype(
        jnp.bfloat16
    )
    head_grad = lax.dot_general(
        normed_all, score_grad, (((0,), (0,)), ((), ())), preferred_element_type=jnp.float32
    )
    partial_grad = lax.psum_scatter(
        lax.dot_general(
            score_grad, head_weight, (((1,), (1,)), ((), ())), preferred_element_type=jnp.float32
        ),
        "expert",
        scatter_dimension=0,
        tiled=True,
    )
    normed_grad = lax.psum(partial_grad, "vocab")
    gained = final_gain[None, :] * normed_grad
    residual_full = (
        gained - unit_rows * jnp.mean(unit_rows * gained, axis=1, keepdims=True)
    ) / row_scale
    feature_start = lax.axis_index("vocab") * feature_share
    residual_grad = lax.dynamic_slice_in_dim(residual_full, feature_start, feature_share, 1)
    flat_ids = expert_ids.reshape(-1)
    labels = jnp.arange(experts_all, dtype=jnp.int32)
    onehot = (flat_ids[:, None] == labels[None, :]).astype(jnp.int32)
    earlier = jnp.cumsum(onehot, axis=0) - onehot
    slot_index = jnp.sum(earlier * onehot, axis=1)
    position = flat_ids * capacity + slot_index
    routed_grad = (
        (gate_weights[:, :, None] * residual_full[:, None, :])
        .astype(jnp.bfloat16)
        .reshape(-1, model_width)
    )
    inputs_rep = jnp.repeat(moe_input, top_count, axis=0)
    buffer_rows = experts_all * capacity
    send_inputs = (
        jnp.zeros((buffer_rows, model_width), jnp.bfloat16)
        .at[position]
        .set(inputs_rep)
        .reshape(experts_all, capacity, model_width)
    )
    send_grads = (
        jnp.zeros((buffer_rows, model_width), jnp.bfloat16)
        .at[position]
        .set(routed_grad)
        .reshape(experts_all, capacity, model_width)
    )
    part_inputs = lax.dynamic_slice_in_dim(send_inputs, feature_start, feature_share, 2)
    part_grads = lax.dynamic_slice_in_dim(send_grads, feature_start, feature_share, 2)
    moved_inputs, moved_grads = (
        lax.all_to_all(part_inputs, "expert", split_axis=0, concat_axis=1, tiled=True),
        lax.all_to_all(part_grads, "expert", split_axis=0, concat_axis=1, tiled=True),
    )
    inputs_slot, grads_slot = (
        lax.all_gather(moved_inputs, "vocab", axis=2, tiled=True),
        lax.all_gather(moved_grads, "vocab", axis=2, tiled=True),
    )
    gate_pre = jnp.einsum("esd,edf->esf", inputs_slot, w_gate, preferred_element_type=jnp.float32)
    up_pre = jnp.einsum("esd,edf->esf", inputs_slot, w_up, preferred_element_type=jnp.float32)
    act_grad = jnp.einsum("esd,efd->esf", grads_slot, w_down, preferred_element_type=jnp.float32)
    sigmoid_gate = jax.nn.sigmoid(gate_pre)
    gate_grad = (act_grad * up_pre * sigmoid_gate * (1.0 + gate_pre * (1.0 - sigmoid_gate))).astype(
        jnp.bfloat16
    )
    up_grad = (act_grad * gate_pre * sigmoid_gate).astype(jnp.bfloat16)
    partial_input = jnp.einsum(
        "esf,edf->esd", gate_grad, w_gate, preferred_element_type=jnp.float32
    )
    partial_input = partial_input + jnp.einsum(
        "esf,edf->esd", up_grad, w_up, preferred_element_type=jnp.float32
    )
    slot_share = lax.psum_scatter(partial_input, "vocab", scatter_dimension=2, tiled=True)
    returned = lax.all_to_all(slot_share, "expert", split_axis=1, concat_axis=0, tiled=True)
    per_pair = returned.reshape(-1, feature_share)[position]
    input_grad = jnp.sum(per_pair.reshape(rows_local, top_count, feature_share), axis=1)
    return (head_grad, residual_grad, input_grad)


def solution(mesh):
    in_specs = (
        P("expert", None),
        P("expert", None),
        P(),
        P(None, ("expert", "vocab")),
        P("expert"),
        P("expert"),
        P(),
        P("expert", None),
        P("expert", None),
        P("expert", None, "vocab"),
        P("expert", None, "vocab"),
        P("expert", "vocab", None),
    )
    out_specs = (P(None, ("expert", "vocab")), P("expert", "vocab"), P("expert", "vocab"))
    return jax.shard_map(
        on_device, mesh=mesh, in_specs=in_specs, out_specs=out_specs, check_vma=False
    )
```

profile of v0, /device:TPU:0, one launch (start us, length us, event | category | flops | bytes accessed | tf_op | source)
XLA Modules:
  0.0 321.3 jit_solution(14341958270852453572)
XLA Ops:
  7.2 1.2 fusion.20
  8.4 1.7 multiply_convert_fusion.2
  10.2 1.2 dynamic-slice
  12.1 0.9 dynamic-update-slice
  13.0 0.8 dynamic-update-slice.1
  13.8 13.1 %all-reduce.2 = (s32[256]{0:T(256)S(1)}, s32[256]{0:T(256)S(1)}) all-reduce(s32[256]{0:T(256)S(1)} %dynamic-update-slice.1, s32[256]{0:T(256)S(1)} %dynamic-update-slice), channel_id=1, replica_groups=mesh['expert'=8,'vocab'=4] {'expert'}, use_global_device_ids=true, to_apply=%add.1 | all-reduce | flops 512 | bytes 4096
  26.9 0.7 select_reduce_fusion
  27.7 26.3 %all-gather.4.cloned.1.call-done = bf16[256,2048]{1,0:T(8,128)(2,1)} async-done(((bf16[32,2048]{1,0:T(8,128)(2,1)}), bf16[256,2048]{1,0:T(8,128)(2,1)}) %all-gather.4.cloned.1.call-update) | async-done | bytes 1048592 | tf_op jit(solution)/shard_map/all_gather | solution.py:40
  53.9 2.6 fusion.6
  56.5 0.7 copy-done.4
  57.2 2.1 fusion.30
  59.3 0.1 copy.34
  59.4 0.1 eq.61
  59.4 0.1 eq.57
  59.5 0.6 reduce-window.6
  60.1 0.2 slice_reduce_fusion
  60.4 0.1 copy.33
  60.4 0.1 mul.122
  60.6 0.1 fusion.25
  60.7 3.7 %scatter_custom_fusion.1 = bf16[512,2048]{1,0:T(8,128)(2,1)} fusion(s32[256]{0:T(256)S(1)} %bitcast.68, bf16[]{:T(256)} %constant.39.clone.1, bf16[32,2048]{1,0:T(8,128)(2,1)S(1)} %copy-done.5), kind=kCustom, calls=%fused_computation.16 | custom fusion | bytes 2228226 | tf_op jit(solution)/shard_map/scatter | solution.py:90
  64.4 2.0 constant_dynamic-slice_fusion
  66.4 3.5 %all-to-all-start.1 = ((bf16[16,32,512]{2,1,0:T(8,128)(2,1)}), bf16[16,32,512]{2,1,0:T(8,128)(2,1)S(1)}, u32[]{:S(2)}, u32[]{:S(2)}) async-start(bf16[16,32,512]{2,1,0:T(8,128)(2,1)} %constant_dynamic-slice_fusion), calls=%async_computation.2 | async-start | bytes 1048576 | tf_op jit(solution)/shard_map/all_to_all | solution.py:102
  70.0 64.0 %reduce-scatter.3.cloned.1.call-done = f32[32,2048]{1,0:T(8,128)} async-done(((f32[256,2048]{1,0:T(8,128)}), f32[32,2048]{1,0:T(8,128)}) %reduce-scatter.3.cloned.1.call-update) | async-done | bytes 262160 | tf_op jit(solution)/shard_map/reduce_scatter | solution.py:59
  134.0 0.8 copy.39
  135.0 0.1 mul.124
  135.1 32.5 %all-reduce.5.cloned.1.call-done = f32[32,2048]{1,0:T(8,128)} async-done(((f32[32,2048]{1,0:T(8,128)}), f32[32,2048]{1,0:T(8,128)}) %all-reduce.5.cloned.1.call-update) | async-done | bytes 262160 | tf_op jit(solution)/shard_map/psum | solution.py:67
  167.6 1.2 multiply_reduce_fusion
  168.8 1.1 subtract_divide_fusion
  169.9 3.8 %scatter_custom_fusion = bf16[512,2048]{1,0:T(8,128)(2,1)} fusion(s32[256]{0:T(256)S(1)} %bitcast.69, f32[32,2048]{1,0:T(8,128)S(1)} %subtract_divide_fusion, f32[256]{0:T(256)S(1)} %mul.124, bf16[]{:T(256)} %constant.39.clone.1), kind=kCustom, calls=%fused_computation.15 | custom fusion | flops 1048576 | bytes 2360322 | tf_op jit(solution)/shard_map/scatter | solution.py:96
  173.7 1.1 constant_dynamic-slice_fusion.1
  174.7 18.6 %all_to_all.51 = bf16[16,32,512]{2,1,0:T(8,128)(2,1)S(1)} all-to-all(bf16[16,32,512]{2,1,0:T(8,128)(2,1)S(1)} %constant_dynamic-slice_fusion.1), channel_id=1, replica_groups=mesh['expert'=8,'vocab'=4] {'expert'}, dimensions={0} | all-to-all | bytes 1048576 | tf_op jit(solution)/shard_map/all_to_all | solution.py:103
  193.4 0.8 copy.38
  194.2 0.2 reduce-scatter.5.cloned.1.call-start
  194.5 2.9 fusion.32
  197.4 18.8 %all-gather.6.cloned.1.call-done = bf16[2,256,2048]{2,1,0:T(8,128)(2,1)} async-done(((bf16[2,256,512]{2,1,0:T(8,128)(2,1)}), bf16[2,256,2048]{2,1,0:T(8,128)(2,1)}) %all-gather.6.cloned.1.call-update) | async-done | bytes 2097168 | tf_op jit(solution)/shard_map/all_gather | solution.py:107
  216.2 3.0 fusion.31
  219.2 5.6 %fusion.7 = f32[2,256,2048]{2,1,0:T(8,128)} fusion(bf16[2,2048,256]{2,1,0:T(8,128)(2,1)} %param.21, f32[2,256,256]{2,1,0:T(8,128)S(1)} %fusion.31, bf16[2,256,2048]{2,1,0:T(8,128)(2,1)} %all-gather.8.cloned.1.call-done, bf16[2,2048,256]{2,1,0:T(8,128)(2,1)S(1)} %copy-done, f32[2,256,256]{2,1,0:T(8,128)S(1)} %fusion.32), kind=kOutput, calls=%fused_computation.14 | convolution fusion | flops 1075052544 | bytes 11534336 | tf_op jit(solution)/shard_map/esf,edf->esd/dot_general | solution.py:117
  224.8 4.9 %convolution_add_fusion = f32[2,256,2048]{2,1,0:T(8,128)} fusion(f32[2,256,2048]{2,1,0:T(8,128)} %fusion.7, bf16[2,2048,256]{2,1,0:T(8,128)(2,1)S(1)} %copy-done, f32[2,256,256]{2,1,0:T(8,128)S(1)} %fusion.31, f32[2,256,256]{2,1,0:T(8,128)S(1)} %fusion.32), kind=kOutput, calls=%fused_computation.3 | convolution fusion | flops 538705920 | bytes 11534336 | tf_op jit(solution)/shard_map/esf,edf->esd/dot_general | solution.py:120
  229.7 44.6 %reduce-scatter.5.cloned.1.call-done = f32[2,256,512]{2,1,0:T(8,128)} async-done(((f32[2,256,2048]{2,1,0:T(8,128)}), f32[2,256,512]{2,1,0:T(8,128)}) %reduce-scatter.5.cloned.1.call-update) | async-done | bytes 1048592 | tf_op jit(solution)/shard_map/reduce_scatter | solution.py:123
  274.2 3.0 copy.40
  277.3 5.5 %all-to-all-start.2 = ((f32[2,256,512]{2,0,1:T(2,128)}), f32[2,256,512]{2,0,1:T(2,128)S(1)}, u32[]{:S(2)}, u32[]{:S(2)}) async-start(f32[2,256,512]{2,0,1:T(2,128)} %copy.40), calls=%async_computation.4 | async-start | bytes 2097152 | tf_op jit(solution)/shard_map/all_to_all | solution.py:124
  282.8 3.7 %fusion.29 = f32[2048,384]{1,0:T(8,128)} fusion(bf16[256,2048]{1,0:T(8,128)(2,1)} %all-gather.4.cloned.1.call-done, bf16[256,384]{1,0:T(8,128)(2,1)} %copy-done.4), kind=kOutput, calls=%fused_computation.59 | convolution fusion | flops 402653184 | bytes 4390912 | tf_op jit(solution)/shard_map/dot_general | solution.py:56
  286.5 0.6 constant_dynamic-slice_fusion.2
  287.1 21.4 %all-to-all-done.2 = f32[2,256,512]{2,0,1:T(2,128)S(1)} async-done(((f32[2,256,512]{2,0,1:T(2,128)}), f32[2,256,512]{2,0,1:T(2,128)S(1)}, u32[]{:S(2)}, u32[]{:S(2)}) %all-to-all-start.2) | async-done | bytes 1048608 | tf_op jit(solution)/shard_map/all_to_all | solution.py:124
  308.5 1.0 copy-done.1
  309.4 1.4 copy.41
  310.9 1.8 gather_fusion
  312.6 1.8 bitcast_reduce_fusion
  (41 shorter events, 0.5 us)
Async XLA Ops:
  7.2 212.0 %copy-start = (bf16[2,2048,256]{2,1,0:T(8,128)(2,1)S(1)}, bf16[2,2048,256]{2,1,0:T(8,128)(2,1)}, u32[]{:S(2)}) copy-start(bf16[2,2048,256]{2,1,0:T(8,128)(2,1)} %param.22) | copy-start | bytes 6291460
  7.2 46.7 %all-gather.4.cloned.1.call-start = ((), (), s32[]{:S(2)}) async-start(), calls=%async_computation.5 | async-start | bytes 1179648 | tf_op jit(solution)/shard_map/all_gather | solution.py:40
  10.1 123.8 %reduce-scatter.3.cloned.1.call-start = ((), (), s32[]{:S(2)}) async-start(), calls=%async_computation.6 | async-start | bytes 2359296 | tf_op jit(solution)/shard_map/reduce_scatter | solution.py:59
  53.9 3.3 %copy-start.3 = (bf16[2048,384]{1,0:T(8,128)(2,1)S(1)}, bf16[2048,384]{1,0:T(8,128)(2,1)}, u32[]{:S(2)}) copy-start(bf16[2048,384]{1,0:T(8,128)(2,1)} %param.15) | copy-start | bytes 4718596
  56.5 0.7 copy-start.4
  57.2 2.1 copy-start.7
  59.2 1.4 copy-start.5
  64.4 70.6 %copy-start.8 = (f32[32,8]{0,1:T(8,128)S(1)}, f32[32,8]{0,1:T(8,128)}, u32[]{:S(2)}) copy-start(f32[32,8]{0,1:T(8,128)} %param.19) | copy-start | bytes 3076
  64.4 103.2 %copy-start.2 = (bf16[32,2048]{1,0:T(8,128)(2,1)S(1)}, bf16[32,2048]{1,0:T(8,128)(2,1)}, u32[]{:S(2)}) copy-start(bf16[32,2048]{1,0:T(8,128)(2,1)} %param.12) | copy-start | bytes 393220
  64.4 103.2 %copy-start.6 = (f32[2048]{0:T(1024)S(1)}, f32[2048]{0:T(1024)}, u32[]{:S(2)}) copy-start(f32[2048]{0:T(1024)} %param.14) | copy-start | bytes 24580
  66.4 67.6 %all-to-all-start.1 = ((bf16[16,32,512]{2,1,0:T(8,128)(2,1)}), bf16[16,32,512]{2,1,0:T(8,128)(2,1)S(1)}, u32[]{:S(2)}, u32[]{:S(2)}) async-start(bf16[16,32,512]{2,1,0:T(8,128)(2,1)} %constant_dynamic-slice_fusion), calls=%async_computation.2 | async-start | bytes 1048576 | tf_op jit(solution)/shard_map/all_to_all | solution.py:102
  69.9 97.7 %all-reduce.5.cloned.1.call-start = ((), (), s32[]{:S(2)}) async-start(), calls=%async_computation.7 | async-start | bytes 524288 | tf_op jit(solution)/shard_map/psum | solution.py:67
  134.0 60.5 %all-gather.8.cloned.1.call-start = ((), (), s32[]{:S(2)}) async-start(), calls=%async_computation.9 | async-start | bytes 2621440 | tf_op jit(solution)/shard_map/all_gather | solution.py:106
  134.9 81.3 %all-gather.6.cloned.1.call-start = ((), (), s32[]{:S(2)}) async-start(), calls=%async_computation.8 | async-start | bytes 2621440 | tf_op jit(solution)/shard_map/all_gather | solution.py:107
  194.2 80.0 %reduce-scatter.5.cloned.1.call-start = ((), (), s32[]{:S(2)}) async-start(), calls=%async_computation.10 | async-start | bytes 5242880 | tf_op jit(solution)/shard_map/reduce_scatter | solution.py:123
  277.3 31.2 %all-to-all-start.2 = ((f32[2,256,512]{2,0,1:T(2,128)}), f32[2,256,512]{2,0,1:T(2,128)S(1)}, u32[]{:S(2)}, u32[]{:S(2)}) async-start(f32[2,256,512]{2,0,1:T(2,128)} %copy.40), calls=%async_computation.4 | async-start | bytes 2097152 | tf_op jit(solution)/shard_map/all_to_all | solution.py:124
  308.4 1.0 copy-start.1
Sparse Core Ops, SparseCore 0:
  10.7 43.1 all-gather.3
  59.4 74.5 reduce-scatter.2
  136.3 31.2 all-reduce.4
  169.0 22.5 all-gather.7
  194.4 21.8 all-gather.5
  229.8 44.4 reduce-scatter.4
where the time goes:
time: 322 us; the launch traced here: 321 us
  waiting for transfers between devices  208 us (65%)
  blocking collectives  31.8 us (10%)
  matrix products  24.6 us (8%)
  local copies, waits for them, and re-layouts  20.8 us (6%)
  between operations  14.9 us (5%)
  other arithmetic  12.2 us (4%)
  starting transfers between devices  9.43 us (3%)
    reduce_scatter x1, waiting for transfers between devices, on_device(): lax.psum_scatter(lax.dot_general(score_grad, head_weight, (((1,), (1,)),...  64 us
    reduce_scatter x1, waiting for transfers between devices, on_device(): lax.psum_scatter(partial_input, 'vocab', scatter_dimension=2, tiled=True)  44.6 us
    psum x1, waiting for transfers between devices, on_device(): normed_grad = lax.psum(partial_grad, 'vocab')  32.5 us
    all_gather x1, waiting for transfers between devices, on_device(): lax.all_gather(normed, 'expert', axis=0, tiled=True)  26.3 us
    all_to_all x1, waiting for transfers between devices, on_device(): lax.all_to_all(slot_share, 'expert', split_axis=1, concat_axis=0, tiled=T...  21.4 us
    all_gather x1, waiting for transfers between devices, on_device(): lax.all_gather(moved_grads, 'vocab', axis=2, tiled=True)  18.8 us
    all_to_all x1, blocking collectives, on_device(): lax.all_to_all(part_grads, 'expert', split_axis=0, concat_axis=1, tiled=T...  18.6 us
    unnamed x1, blocking collectives  13.1 us
  transfers between devices with their start and end apart: 8, of which 6 were waited for; matrix products, arithmetic and copies ran while one was open for 8% of the time, Pallas kernels for 0%

commit v1 on v0

v1 whole, which is shorter than its diff:
```python
import functools
import math

import jax
import jax.numpy as jnp
from jax import lax
from jax.experimental import pallas as pl
from jax.experimental.pallas import tpu as pltpu
from jax.sharding import PartitionSpec as P

epsilon = 1e-05
CORES = 2
MESH = pl.DeviceIdType.MESH
VMEM = pl.BlockSpec(memory_space=pltpu.VMEM)


def place():
    e, v = lax.axis_index("expert"), lax.axis_index("vocab")
    n_expert, n_vocab = lax.axis_size("expert"), lax.axis_size("vocab")
    return e, v // CORES, v % CORES, n_expert, n_vocab // CORES


def device(e, a, c):
    return (e, a * CORES + c)


def greet(devices):
    barrier = pltpu.get_barrier_semaphore()
    for other in devices:
        pl.semaphore_signal(barrier, inc=1, device_id=other, device_id_type=MESH)
    pl.semaphore_wait(barrier, len(devices))


def remote(src, dst, send, recv, target):
    return pltpu.make_async_remote_copy(
        src_ref=src, dst_ref=dst, send_sem=send, recv_sem=recv, device_id=target,
        device_id_type=MESH,
    )


def gather_kernel(n_data, n_meta, *refs):
    count = n_data + n_meta
    ins, outs = refs[:count], refs[count:2 * count]
    local_sem, e_send, e_recv, a_send, a_recv, c_send, c_recv, m_send, m_recv = refs[2 * count:]
    e, a, c, n_e, n_a = place()
    expert_peer = [device(lax.rem(e + d, n_e), a, c) for d in range(1, n_e)]
    chip_peer = [device(e, lax.rem(a + d, n_a), c) for d in range(1, n_a)]
    sibling = device(e, a, 1 - c)
    greet(expert_peer + chip_peer + [sibling])
    share = ins[0].shape[1]

    def block(i, eb, ab, cb):
        start = pl.multiple_of((ab * CORES + cb) * share, share)
        return outs[i].at[eb, :, pl.ds(start, share)]

    sends = []

    def start(*args):
        copy = remote(*args)
        copy.start()
        sends.append(copy)

    locals_ = []
    for m in range(n_meta):
        i = n_data + m
        for d in range(1, n_e):
            start(ins[i], outs[i].at[e], m_send.at[m, d], m_recv.at[m, d], expert_peer[d - 1])
        own = pltpu.make_async_copy(ins[i], outs[i].at[e], local_sem.at[i])
        own.start()
        locals_.append(own)
    for i in range(n_data):
        for d in range(1, n_e):
            start(ins[i], block(i, e, a, c), e_send.at[i, d], e_recv.at[i, d], expert_peer[d - 1])
        own = pltpu.make_async_copy(ins[i], block(i, e, a, c), local_sem.at[i])
        own.start()
        locals_.append(own)
    for i in range(n_data):
        for d in range(n_e):
            eb = lax.rem(e + n_e - d, n_e)
            mine = block(i, eb, a, c)
            if d:
                remote(mine, mine, e_send.at[i, d], e_recv.at[i, d], sibling).wait_recv()
            src = mine if d else ins[i]
            for da in range(1, n_a):
                start(src, mine, a_send.at[i, d, da], a_recv.at[i, d, da], chip_peer[da - 1])
            start(src, mine, c_send.at[i, d, 0], c_recv.at[i, d, 0], sibling)
    for i in range(n_data):
        for d in range(n_e):
            eb = lax.rem(e + n_e - d, n_e)
            for da in range(1, n_a):
                other = block(i, eb, lax.rem(a + n_a - da, n_a), c)
                remote(other, other, a_send.at[i, d, da], a_recv.at[i, d, da], sibling).wait_recv()
                start(other, other, c_send.at[i, d, da], c_recv.at[i, d, da], sibling)
    for own in locals_:
        own.wait()
    for m in range(n_meta):
        for d in range(1, n_e):
            slot = outs[n_data + m].at[lax.rem(e + n_e - d, n_e)]
            remote(slot, slot, m_send.at[m, d], m_recv.at[m, d], sibling).wait_recv()
    for i in range(n_data):
        for d in range(n_e):
            eb = lax.rem(e + n_e - d, n_e)
            for da in range(n_a):
                other = block(i, eb, lax.rem(a + n_a - da, n_a), 1 - c)
                remote(other, other, c_send.at[i, d, da], c_recv.at[i, d, da], sibling).wait_recv()
    for copy in sends:
        copy.wait_send()


def gather_all(data, meta, collective_id):
    n_e, n_a = lax.axis_size("expert"), lax.axis_size("vocab") // CORES
    n_data, n_meta = len(data), len(meta)
    width = data[0].shape[1] * n_a * CORES
    out_shape = [jax.ShapeDtypeStruct((n_e, x.shape[0], width), x.dtype) for x in data]
    out_shape += [jax.ShapeDtypeStruct((n_e, *x.shape), x.dtype) for x in meta]
    dma = pltpu.SemaphoreType.DMA
    more = max(n_meta, 1)
    outs = pl.pallas_call(
        functools.partial(gather_kernel, n_data, n_meta),
        out_shape=out_shape,
        in_specs=[VMEM] * (n_data + n_meta),
        out_specs=[VMEM] * (n_data + n_meta),
        scratch_shapes=[
            dma((n_data + n_meta,)),
            dma((n_data, n_e)), dma((n_data, n_e)),
            dma((n_data, n_e, n_a)), dma((n_data, n_e, n_a)),
            dma((n_data, n_e, n_a)), dma((n_data, n_e, n_a)),
            dma((more, n_e)), dma((more, n_e)),
        ],
        compiler_params=pltpu.CompilerParams(collective_id=collective_id, has_side_effects=True),
    )(*data, *meta)
    return [x.reshape(-1, x.shape[-1]) for x in outs]


def core_kernel(x_ref, y_ref, send, recv):
    e, a, c, _, n_a = place()
    sibling = device(e, a, 1 - c)
    greet([sibling])
    share = y_ref.shape[2]
    copies = []
    for k in range(n_a):
        start = pl.multiple_of((k * CORES + 1 - c) * share, share)
        copy = remote(x_ref.at[:, pl.ds(start, share)], y_ref.at[k], send.at[k], recv.at[k], sibling)
        copy.start()
        copies.append(copy)
    for copy in copies:
        copy.wait()


def core_swap(x, collective_id):
    n_a = lax.axis_size("vocab") // CORES
    share = x.shape[1] // (n_a * CORES)
    dma = pltpu.SemaphoreType.DMA
    return pl.pallas_call(
        core_kernel,
        out_shape=jax.ShapeDtypeStruct((n_a, x.shape[0], share), x.dtype),
        in_specs=[VMEM],
        out_specs=VMEM,
        scratch_shapes=[dma((n_a,)), dma((n_a,))],
        compiler_params=pltpu.CompilerParams(collective_id=collective_id, has_side_effects=True),
    )(x)


def swap_kernel(kind, n, x_ref, y_ref, send, recv):
    e, a, c, _, _ = place()
    me = {"expert": e, "chip": a, "vocab": a * CORES + c}[kind]
    others = [lax.rem(me + d, n) for d in range(1, n)]

    def at(p):
        if kind == "expert":
            return device(p, a, c)
        return device(e, p, c) if kind == "chip" else (e, p)

    greet([at(p) for p in others])
    copies = []
    for d, p in enumerate(others):
        src = x_ref if kind == "vocab" else x_ref.at[p]
        copy = remote(src, y_ref.at[d], send.at[d], recv.at[d], at(p))
        copy.start()
        copies.append(copy)
    for copy in copies:
        copy.wait()


def swap(x, kind, n, collective_id):
    block = x.shape if kind == "vocab" else x.shape[1:]
    dma = pltpu.SemaphoreType.DMA
    return pl.pallas_call(
        functools.partial(swap_kernel, kind, n),
        out_shape=jax.ShapeDtypeStruct((n - 1, *block), x.dtype),
        in_specs=[VMEM],
        out_specs=VMEM,
        scratch_shapes=[dma((n - 1,)), dma((n - 1,))],
        compiler_params=pltpu.CompilerParams(collective_id=collective_id, has_side_effects=True),
    )(x)


def scatter_sum(partial, chip_type, expert_type, first_id):
    e, a, c, n_e, n_a = place()
    rows, width = partial.shape
    share = width // (n_a * CORES)
    other = core_swap(partial, first_id)
    by_chip = jnp.stack([
        lax.dynamic_slice_in_dim(partial, (k * CORES + c) * share, share, 1) + other[k]
        for k in range(n_a)
    ])
    arrived = swap(by_chip.astype(chip_type), "chip", n_a, first_id + 1)
    total = lax.dynamic_index_in_dim(by_chip, a, 0, False)
    total = total + jnp.sum(arrived.astype(jnp.float32), axis=0)
    by_row = total.reshape(n_e, rows // n_e, share)
    arrived = swap(by_row.astype(expert_type), "expert", n_e, first_id + 2)
    own = lax.dynamic_index_in_dim(by_row, e, 0, False)
    return own + jnp.sum(arrived.astype(jnp.float32), axis=0)


def on_device(
    layer_out,
    moe_input,
    final_gain,
    head_weight,
    clean_ids,
    levels,
    ratio_table,
    gate_weights,
    expert_ids,
    w_gate,
    w_up,
    w_down,
):
    rows_local, model_width = layer_out.shape
    n_expert = lax.axis_size("expert")
    n_vocab = lax.axis_size("vocab")
    expert_at, vocab_at = lax.axis_index("expert"), lax.axis_index("vocab")
    total_rows = rows_local * n_expert
    local_experts = w_gate.shape[0]
    experts_all = local_experts * n_expert
    share = model_width // n_vocab
    vocab_local = head_weight.shape[1]

    def own_share(x, axis):
        return lax.dynamic_slice_in_dim(x, vocab_at * share, share, axis)

    values = layer_out.astype(jnp.float32)
    row_scale = jnp.sqrt(jnp.mean(values * values, axis=1, keepdims=True) + epsilon)
    unit_share = own_share(layer_out, 1).astype(jnp.float32) / row_scale
    gain_share = own_share(final_gain, 0)[None, :]
    normed_share = (unit_share * gain_share).astype(jnp.bfloat16)
    labels = jnp.arange(experts_all, dtype=jnp.int32)
    gates = jnp.sum(
        jnp.where(expert_ids[:, :, None] == labels, gate_weights[:, :, None], 0.0), axis=1
    )
    level_labels = jnp.arange(ratio_table.shape[0], dtype=jnp.int32)
    ratio_rows = jnp.sum(
        jnp.where(levels[:, None] == level_labels[None, :], ratio_table[None, :], 0.0),
        axis=1, keepdims=True,
    )
    meta = jnp.concatenate([gates, ratio_rows, clean_ids[:, None].astype(jnp.float32)], axis=1)
    meta = jnp.pad(meta, ((0, 0), (0, -meta.shape[1] % 128)))
    normed_all, input_all, meta_all = gather_all(
        [normed_share, own_share(moe_input, 1)], [meta], 0
    )
    ratio_all = meta_all[:, experts_all:experts_all + 1]
    clean_all = meta_all[:, experts_all + 1:experts_all + 2].astype(jnp.int32)
    gate_all = lax.dynamic_slice_in_dim(meta_all, expert_at * local_experts, local_experts, 1)

    column_start = (expert_at * n_vocab + vocab_at) * vocab_local
    columns = column_start + jnp.arange(vocab_local, dtype=jnp.int32)
    scores = jnp.dot(normed_all, head_weight, preferred_element_type=jnp.float32)
    target_hit = (clean_all == columns[None, :]).astype(jnp.float32)
    loss_scale = 1.0 / math.sqrt(total_rows)
    score_grad = ((jnp.exp(scores) - ratio_all * target_hit) * loss_scale).astype(jnp.bfloat16)
    head_grad = lax.dot_general(
        normed_all, score_grad, (((0,), (0,)), ((), ())), preferred_element_type=jnp.float32
    )
    partial_grad = lax.dot_general(
        score_grad, head_weight, (((1,), (1,)), ((), ())), preferred_element_type=jnp.float32
    )
    normed_grad = scatter_sum(partial_grad, jnp.bfloat16, jnp.bfloat16, 1)
    gained = gain_share * normed_grad
    mean_part = jnp.sum(unit_share * gained, axis=1, keepdims=True) / model_width
    mean_part = jnp.broadcast_to(mean_part, (rows_local, 128))
    mean_row = mean_part + jnp.sum(swap(mean_part, "vocab", n_vocab, 4), axis=0)
    residual_grad = (gained - unit_share * mean_row[:, :1]) / row_scale
    (residual_all,) = gather_all([residual_grad.astype(jnp.bfloat16)], [], 5)

    partial_input = None
    for i in range(local_experts):
        gate_pre = jnp.dot(input_all, w_gate[i], preferred_element_type=jnp.float32)
        up_pre = jnp.dot(input_all, w_up[i], preferred_element_type=jnp.float32)
        act_grad = gate_all[:, i:i + 1] * lax.dot_general(
            residual_all, w_down[i], (((1,), (1,)), ((), ())), preferred_element_type=jnp.float32
        )
        s = jax.nn.sigmoid(gate_pre)
        gate_grad = (act_grad * up_pre * s * (1.0 + gate_pre * (1.0 - s))).astype(jnp.bfloat16)
        up_grad = (act_grad * gate_pre * s).astype(jnp.bfloat16)
        for grad, weight in ((gate_grad, w_gate[i]), (up_grad, w_up[i])):
            term = lax.dot_general(
                grad, weight, (((1,), (1,)), ((), ())), preferred_element_type=jnp.float32
            )
            partial_input = term if partial_input is None else partial_input + term
    input_grad = scatter_sum(partial_input, jnp.float32, jnp.bfloat16, 6)
    return (head_grad, residual_grad, input_grad)


def solution(mesh):
    in_specs = (
        P("expert", None),
        P("expert", None),
        P(),
        P(None, ("expert", "vocab")),
        P("expert"),
        P("expert"),
        P(),
        P("expert", None),
        P("expert", None),
        P("expert", None, "vocab"),
        P("expert", None, "vocab"),
        P("expert", "vocab", None),
    )
    out_specs = (P(None, ("expert", "vocab")), P("expert", "vocab"), P("expert", "vocab"))
    return jax.shard_map(
        on_device, mesh=mesh, in_specs=in_specs, out_specs=out_specs, check_vma=False
    )
```

time: 322 us -> 169 us (0.52)
  waiting for transfers between devices: 208 us -> 0 us
  Pallas kernels: 0 us -> 112 us
  blocking collectives: 31.8 us -> 0 us
  local copies, waits for them, and re-layouts: 20.8 us -> 4.52 us
  between operations: 14.9 us -> 0.86 us
  other arithmetic: 12.2 us -> 22.6 us
  starting transfers between devices: 9.43 us -> 0 us
  matrix products: 24.6 us -> 28 us
    pallas_call x0 -> x9, Pallas kernels: none -> 112 us  [the longest x5 53.8 us: swap(): pl.pallas_call(functools.partial(swap_kernel, kind, n), out_shape=jax.Sha...]
    reduce_scatter x2 -> x0, waiting for transfers between devices: 109 us -> none  [the longest x1 64 us: on_device(): lax.psum_scatter(lax.dot_general(score_grad, head_weight, (((1,), (1,)),...]
    all_gather x3 -> x0, waiting for transfers between devices: 45.1 us -> none  [the longest x1 26.3 us: on_device(): lax.all_gather(normed, 'expert', axis=0, tiled=True)]
    psum x1 -> x0, waiting for transfers between devices: 32.5 us -> none  [on_device(): normed_grad = lax.psum(partial_grad, 'vocab')]
    all_to_all x2 -> x0, waiting for transfers between devices: 21.4 us -> none  [the longest x1 21.4 us: on_device(): lax.all_to_all(slot_share, 'expert', split_axis=1, concat_axis=0, tiled=T...]
    all_to_all x1 -> x0, blocking collectives: 18.6 us -> none  [on_device(): lax.all_to_all(part_grads, 'expert', split_axis=0, concat_axis=1, tiled=T...]
    unnamed x1 -> x0, blocking collectives: 13.1 us -> none
    all_to_all x2 -> x0, starting transfers between devices: 9.01 us -> none  [the longest x1 5.52 us: on_device(): lax.all_to_all(slot_share, 'expert', split_axis=1, concat_axis=0, tiled=T...]
  transfers between devices with their start and end apart: 8 -> 0, of which waited for: 6 -> 0; matrix products, arithmetic and copies ran while one was open for 8% -> 0% of each run, Pallas kernels for 0% -> 0%
where the time goes in v1:
time: 169 us; the launch traced here: 168 us
  Pallas kernels  112 us (66%)
  matrix products  28 us (17%)
  other arithmetic  22.6 us (13%)
  local copies, waits for them, and re-layouts  4.52 us (3%)
    pallas_call x5, Pallas kernels, swap(): pl.pallas_call(functools.partial(swap_kernel, kind, n), out_shape=jax.Sha...  53.8 us
    pallas_call x2, Pallas kernels, gather_all(): pl.pallas_call(functools.partial(gather_kernel, n_data, n_meta), out_shap...  47.7 us
    dot_general x4, matrix products, on_device(): lax.dot_general(grad, weight, (((1,), (1,)), ((), ())), preferred_element...  16.4 us
    pallas_call x2, Pallas kernels, core_swap(): pl.pallas_call(core_kernel, out_shape=jax.ShapeDtypeStruct((n_a, x.shape[...  10.7 us
    another operation x3, other arithmetic, scatter_sum(): jnp.stack([lax.dynamic_slice_in_dim(partial, (k * CORES + c) * share, sha...  4.51 us
    dot_general x2, matrix products, on_device(): lax.dot_general(residual_all, w_down[i], (((1,), (1,)), ((), ())), prefer...  4.34 us

profile of v1, /device:TPU:0, one launch (start us, length us, event | category | flops | bytes accessed | tf_op | source)
XLA Modules:
  0.0 168.2 jit_solution(14450451885197192819)
XLA Ops:
  0.7 0.9 dynamic_slice.39
  1.5 1.0 multiply_reduce_fusion
  2.6 1.5 multiply_convert_fusion.4.refs_0_
  4.0 1.4 constant_dynamic-slice_fusion.2.refs_1_
  5.4 0.7 select_reduce_fusion
  6.2 0.8 select_reduce_fusion.1
  7.0 0.1 copy.27
  7.1 0.7 convert_bitcast_fusion
  7.7 0.1 copy.28
  7.8 0.7 select_maximum_fusion.refs_2_
  8.5 30.0 %shard_map.139 = (bf16[8,32,2048]{2,1,0:T(8,128)(2,1)}, bf16[8,32,2048]{2,1,0:T(8,128)(2,1)}, f32[8,32,128]{2,1,0:T(8,128)}) custom-call(bf16[32,512]{1,0:T(8,128)(2,1)} %multiply_convert_fusion.4.refs_0_, bf16[32,512]{1,0:T(8,128)(2,1)} %constant_dynamic-slice_fusion.2.refs_1_, f32[32,128]{1,0:T(8,128)} %select_maximum_fusion.refs_2_), custom_call_target="tpu_custom_call" | custom-call | tf_op jit(solution)/shard_map/pallas_call | solution.py:118
  38.5 2.0 %constant_dynamic-slice_fusion = (f32[256,1]{1,0:T(8,128)S(1)}, f32[256,1]{1,0:T(8,128)}, f32[256,1]{1,0:T(8,128)S(1)}, s32[256,1]{1,0:T(8,128)S(1)}) fusion(f32[256,128]{1,0:T(8,128)} %bitcast.99, s32[]{:T(128)S(6)} %add.150, s32[]{:T(128)S(6)} %select_n.57), kind=kLoop, calls=%fused_computation.93 | loop fusion | flops 256 | bytes 8200 | tf_op jit(solution)/shard_map/slice | solution.py:290
  40.6 2.0 %fusion.2 = bf16[256,384]{1,0:T(8,128)(2,1)S(1)} fusion(bf16[256,2048]{1,0:T(8,128)(2,1)} %bitcast.92, bf16[2048,384]{1,0:T(8,128)(2,1)S(1)} %copy-done, f32[256]{0:T(256)S(1)} %bitcast.103, s32[384]{0:T(512)S(1)} %iota_add_fusion, s32[256]{0:T(256)S(1)} %bitcast.102), kind=kOutput, calls=%fused_computation.12 | convolution fusion | flops 403144704 | bytes 2821632 | tf_op jit(solution)/shard_map/dot_general | solution.py:268
  42.6 2.1 %fusion.63.x_ref = f32[256,2048]{1,0:T(8,128)} fusion(bf16[256,384]{1,0:T(8,128)(2,1)S(1)} %fusion.2, bf16[2048,384]{1,0:T(8,128)(2,1)S(1)} %copy-done), kind=kOutput, calls=%fused_computation.106 | convolution fusion | flops 402653184 | bytes 3866624 | tf_op jit(solution)/shard_map/dot_general | solution.py:275
  44.7 5.3 %shard_map.140 = f32[2,256,512]{2,1,0:T(8,128)} custom-call(f32[256,2048]{1,0:T(8,128)} %fusion.63.x_ref), custom_call_target="tpu_custom_call" | custom-call | tf_op jit(solution)/shard_map/pallas_call | solution.py:154
  50.0 1.7 %fusion.43 = (f32[1,256,512]{2,1,0:T(8,128)S(1)}, f32[1,256,512]{2,1,0:T(8,128)S(1)}) fusion(f32[2,256,512]{2,1,0:T(8,128)} %shard_map.140, f32[256,2048]{1,0:T(8,128)} %fusion.63.x_ref, s32[]{:T(128)S(6)} %select_n.53, s32[]{:T(128)S(6)} %select_n.52), kind=kLoop, calls=%fused_computation.56 | loop fusion | flops 262144 | bytes 3145736 | tf_op jit(solution)/shard_map/stack | solution.py:203
  51.8 0.9 fusion.10.x_ref
  52.6 10.4 %shard_map.141 = bf16[1,256,512]{2,1,0:T(8,128)(2,1)} custom-call(bf16[2,256,512]{2,1,0:T(8,128)(2,1)} %fusion.10.x_ref), custom_call_target="tpu_custom_call" | custom-call | tf_op jit(solution)/shard_map/pallas_call | solution.py:188
  63.0 1.1 fusion.40
  64.1 0.7 convert_element_type.66.x_ref
  64.8 11.7 %shard_map.142 = bf16[7,32,512]{2,1,0:T(8,128)(2,1)} custom-call(bf16[8,32,512]{2,1,0:T(8,128)(2,1)} %convert_element_type.66.x_ref), custom_call_target="tpu_custom_call" | custom-call | tf_op jit(solution)/shard_map/pallas_call | solution.py:188
  76.5 1.0 convert_reduce_fusion.1
  77.5 1.0 multiply_reduce_fusion.1
  78.5 0.7 broadcast_in_dim.48.x_ref
  79.2 5.1 %shard_map.143 = f32[3,32,128]{2,1,0:T(8,128)} custom-call(f32[32,128]{1,0:T(8,128)} %broadcast_in_dim.48.x_ref), custom_call_target="tpu_custom_call" | custom-call | tf_op jit(solution)/shard_map/pallas_call | solution.py:188
  84.3 0.8 reduce_sum.76
  85.1 0.2 fusion.56
  85.3 1.6 fusion.61
  86.9 17.7 %shard_map.144 = bf16[8,32,2048]{2,1,0:T(8,128)(2,1)} custom-call(bf16[32,512]{1,0:T(8,128)(2,1)} %get-tuple-element.9.refs_0_), custom_call_target="tpu_custom_call" | custom-call | tf_op jit(solution)/shard_map/pallas_call | solution.py:118
  104.6 1.0 copy.35
  105.6 2.2 %convolution_multiply_fusion.3 = f32[256,256]{1,0:T(8,128)S(1)} fusion(bf16[256,2048]{1,0:T(8,128)(2,1)} %bitcast.100, bf16[2,256,2048]{2,1,0:T(8,128)(2,1)} %param.23, f32[256]{0:T(256)S(1)} %bitcast.105), kind=kOutput, calls=%fused_computation.20 | convolution fusion | flops 268500992 | bytes 2360320 | tf_op jit(solution)/shard_map/dot_general | solution.py:290
  107.8 0.4 fusion.19
  108.3 4.1 %fusion.9 = f32[256,2048]{1,0:T(8,128)} fusion(f32[256,256]{1,0:T(8,128)S(1)} %convolution_multiply_fusion.3, bf16[256,2048]{1,0:T(8,128)(2,1)S(1)} %bitcast.89, bf16[2,2048,256]{2,1,0:T(8,128)(2,1)} %param.21, bf16[2,2048,256]{2,1,0:T(8,128)(2,1)} %param.22, f32[256,256]{1,0:T(8,128)S(1)} %fusion.19), kind=kOutput, calls=%fused_computation.23 | convolution fusion | flops 537526272 | bytes 5767168 | tf_op jit(solution)/shard_map/dot_general | solution.py:297
  112.4 3.7 %convolution_add_fusion.2 = f32[256,2048]{1,0:T(8,128)} fusion(f32[256,2048]{1,0:T(8,128)} %fusion.9, bf16[2,2048,256]{2,1,0:T(8,128)(2,1)} %param.22, f32[256,256]{1,0:T(8,128)S(1)} %convolution_multiply_fusion.3, f32[256,256]{1,0:T(8,128)S(1)} %fusion.19), kind=kOutput, calls=%fused_computation.2 | convolution fusion | flops 269352960 | bytes 5767168 | tf_op jit(solution)/shard_map/dot_general | solution.py:297
  116.2 2.2 %convolution_multiply_fusion.1 = f32[256,256]{1,0:T(8,128)S(1)} fusion(bf16[256,2048]{1,0:T(8,128)(2,1)} %bitcast.101, bf16[2,256,2048]{2,1,0:T(8,128)(2,1)} %param.23, f32[256]{0:T(256)S(1)} %bitcast.104), kind=kOutput, calls=%fused_computation.16 | convolution fusion | flops 268500992 | bytes 2360320 | tf_op jit(solution)/shard_map/dot_general | solution.py:290
  118.5 0.4 fusion.12
  118.9 4.8 %convolution_add_fusion.1 = f32[256,2048]{1,0:T(8,128)} fusion(f32[256,2048]{1,0:T(8,128)} %convolution_add_fusion.2, f32[256,256]{1,0:T(8,128)S(1)} %convolution_multiply_fusion.1, bf16[256,2048]{1,0:T(8,128)(2,1)S(1)} %bitcast.91, bf16[2,2048,256]{2,1,0:T(8,128)(2,1)} %param.21, bf16[2,2048,256]{2,1,0:T(8,128)(2,1)} %param.22, f32[256,256]{1,0:T(8,128)S(1)} %fusion.12), kind=kOutput, calls=%fused_computation.1 | convolution fusion | flops 538050560 | bytes 7864320 | tf_op jit(solution)/shard_map/dot_general | solution.py:297
  123.7 3.7 %convolution_add_fusion.x_ref = f32[256,2048]{1,0:T(8,128)} fusion(f32[256,2048]{1,0:T(8,128)} %convolution_add_fusion.1, bf16[2,2048,256]{2,1,0:T(8,128)(2,1)} %param.22, f32[256,256]{1,0:T(8,128)S(1)} %convolution_multiply_fusion.1, f32[256,256]{1,0:T(8,128)S(1)} %fusion.12), kind=kOutput, calls=%fused_computation | convolution fusion | flops 269352960 | bytes 5767168 | tf_op jit(solution)/shard_map/dot_general | solution.py:297
  127.5 5.3 %shard_map.145 = f32[2,256,512]{2,1,0:T(8,128)} custom-call(f32[256,2048]{1,0:T(8,128)} %convolution_add_fusion.x_ref), custom_call_target="tpu_custom_call" | custom-call | tf_op jit(solution)/shard_map/pallas_call | solution.py:154
  132.8 1.7 %fusion.42 = (f32[1,256,512]{2,1,0:T(8,128)S(1)}, f32[1,256,512]{2,1,0:T(8,128)S(1)}) fusion(f32[2,256,512]{2,1,0:T(8,128)} %shard_map.145, f32[256,2048]{1,0:T(8,128)} %convolution_add_fusion.x_ref, s32[]{:T(128)S(6)} %select_n.52, s32[]{:T(128)S(6)} %select_n.53), kind=kLoop, calls=%fused_computation.54 | loop fusion | flops 262144 | bytes 3145736 | tf_op jit(solution)/shard_map/stack | solution.py:203
  134.5 1.0 pad_maximum_fusion.1.x_ref
  135.6 16.3 %shard_map.146 = f32[1,256,512]{2,1,0:T(8,128)} custom-call(f32[2,256,512]{2,1,0:T(8,128)} %pad_maximum_fusion.1.x_ref), custom_call_target="tpu_custom_call" | custom-call | tf_op jit(solution)/shard_map/pallas_call | solution.py:188
  151.8 1.2 fusion.38
  153.1 0.7 convert_element_type.73.x_ref
  153.8 10.3 %shard_map.147 = bf16[7,32,512]{2,1,0:T(8,128)(2,1)} custom-call(bf16[8,32,512]{2,1,0:T(8,128)(2,1)} %convert_element_type.73.x_ref), custom_call_target="tpu_custom_call" | custom-call | tf_op jit(solution)/shard_map/pallas_call | solution.py:188
  164.1 1.0 convert_reduce_fusion
  165.1 0.6 bitcast_add_fusion.4
  165.8 2.4 %fusion.62 = f32[2048,384]{1,0:T(8,128)} fusion(bf16[256,2048]{1,0:T(8,128)(2,1)S(1)} %bitcast.93, bf16[256,384]{1,0:T(8,128)(2,1)S(1)} %fusion.2), kind=kOutput, calls=%fused_computation.105 | convolution fusion | flops 402653184 | bytes 4390912 | tf_op jit(solution)/shard_map/dot_general | solution.py:272
  (17 shorter events, 0.4 us)
Async XLA Ops:
  0.6 40.0 %copy-start = (bf16[2048,384]{1,0:T(8,128)(2,1)S(1)}, bf16[2048,384]{1,0:T(8,128)(2,1)}, u32[]{:S(2)}) copy-start(bf16[2048,384]{1,0:T(8,128)(2,1)} %param.15) | copy-start | bytes 4718596
  85.3 22.5 %copy-start.1 = (bf16[8,32,2048]{2,1,0:T(8,128)(2,1)S(1)}, bf16[8,32,2048]{2,1,0:T(8,128)(2,1)}, u32[]{:S(2)}) copy-start(bf16[8,32,2048]{2,1,0:T(8,128)(2,1)} %get-tuple-element.8) | copy-start | bytes 3145732
  105.6 2.2 %copy-start.3 = (bf16[2,2048,256]{2,1,0:T(8,128)(2,1)S(1)}, bf16[2,2048,256]{2,1,0:T(8,128)(2,1)}, u32[]{:S(2)}) copy-start(bf16[2,2048,256]{2,1,0:T(8,128)(2,1)} %param.21) | copy-start | bytes 6291460
  116.2 2.2 %copy-start.4 = (bf16[2,2048,256]{2,1,0:T(8,128)(2,1)S(1)}, bf16[2,2048,256]{2,1,0:T(8,128)(2,1)}, u32[]{:S(2)}) copy-start(bf16[2,2048,256]{2,1,0:T(8,128)(2,1)} %param.21) | copy-start | bytes 6291460
  153.1 12.7 %copy-start.2 = (bf16[8,32,2048]{2,1,0:T(8,128)(2,1)S(1)}, bf16[8,32,2048]{2,1,0:T(8,128)(2,1)}, u32[]{:S(2)}) copy-start(bf16[8,32,2048]{2,1,0:T(8,128)(2,1)} %get-tuple-element.6) | copy-start | bytes 3145732

commit v2 on v1

--- a/solution.py
+++ b/solution.py
@@ -10,6 +10,7 @@
 
 epsilon = 1e-05
 CORES = 2
+PAIR = 2
 MESH = pl.DeviceIdType.MESH
 VMEM = pl.BlockSpec(memory_space=pltpu.VMEM)
 
@@ -43,66 +44,78 @@
     ins, outs = refs[:count], refs[count:2 * count]
     local_sem, e_send, e_recv, a_send, a_recv, c_send, c_recv, m_send, m_recv = refs[2 * count:]
     e, a, c, n_e, n_a = place()
-    expert_peer = [device(lax.rem(e + d, n_e), a, c) for d in range(1, n_e)]
+    n_o = n_e // PAIR
+    o, inner = e // PAIR, e % PAIR
+    outer_peer = [device(lax.rem(o + d, n_o) * PAIR + inner, a, c) for d in range(1, n_o)]
+    inner_peer = device(o * PAIR + 1 - inner, a, c)
     chip_peer = [device(e, lax.rem(a + d, n_a), c) for d in range(1, n_a)]
     sibling = device(e, a, 1 - c)
-    greet(expert_peer + chip_peer + [sibling])
+    greet(outer_peer + [inner_peer] + chip_peer + [sibling])
     share = ins[0].shape[1]
 
-    def block(i, eb, ab, cb):
+    def source(b):
+        across, d = b // n_o, b % n_o
+        return lax.rem(o + n_o - d, n_o) * PAIR + (1 - inner if across else inner)
+
+    def block(i, b, ab, cb):
         start = pl.multiple_of((ab * CORES + cb) * share, share)
-        return outs[i].at[eb, :, pl.ds(start, share)]
-
-    sends = []
+        return outs[i].at[source(b), :, pl.ds(start, share)]
+
+    sends, locals_ = [], []
 
     def start(*args):
         copy = remote(*args)
         copy.start()
         sends.append(copy)
 
-    locals_ = []
+    def landed(ref, recv):
+        remote(ref, ref, recv, recv, sibling).wait_recv()
+
     for m in range(n_meta):
-        i = n_data + m
-        for d in range(1, n_e):
-            start(ins[i], outs[i].at[e], m_send.at[m, d], m_recv.at[m, d], expert_peer[d - 1])
-        own = pltpu.make_async_copy(ins[i], outs[i].at[e], local_sem.at[i])
+        for d in range(1, n_o):
+            start(ins[n_data + m], outs[n_data + m].at[e], m_send.at[m, d], m_recv.at[m, d],
+                  outer_peer[d - 1])
+    for i in range(count):
+        slot = block(i, 0, a, c) if i < n_data else outs[i].at[e]
+        if i < n_data:
+            for d in range(1, n_o):
+                start(ins[i], slot, e_send.at[i, d], e_recv.at[i, d], outer_peer[d - 1])
+        own = pltpu.make_async_copy(ins[i], slot, local_sem.at[i])
         own.start()
         locals_.append(own)
+    for m in range(n_meta):
+        for d in range(n_o):
+            slot = outs[n_data + m].at[source(d)]
+            if d:
+                landed(slot, m_recv.at[m, d])
+            start(slot if d else ins[n_data + m], slot, m_send.at[m, n_o + d],
+                  m_recv.at[m, n_o + d], inner_peer)
     for i in range(n_data):
-        for d in range(1, n_e):
-            start(ins[i], block(i, e, a, c), e_send.at[i, d], e_recv.at[i, d], expert_peer[d - 1])
-        own = pltpu.make_async_copy(ins[i], block(i, e, a, c), local_sem.at[i])
-        own.start()
-        locals_.append(own)
+        for b in range(n_e):
+            mine = block(i, b, a, c)
+            if b:
+                landed(mine, e_recv.at[i, b])
+            src = mine if b else ins[i]
+            if b < n_o:
+                start(src, mine, e_send.at[i, n_o + b], e_recv.at[i, n_o + b], inner_peer)
+            for da in range(1, n_a):
+                start(src, mine, a_send.at[i, b, da], a_recv.at[i, b, da], chip_peer[da - 1])
+            start(src, mine, c_send.at[i, b, 0], c_recv.at[i, b, 0], sibling)
     for i in range(n_data):
-        for d in range(n_e):
-            eb = lax.rem(e + n_e - d, n_e)
-            mine = block(i, eb, a, c)
-            if d:
-                remote(mine, mine, e_send.at[i, d], e_recv.at[i, d], sibling).wait_recv()
-            src = mine if d else ins[i]
+        for b in range(n_e):
             for da in range(1, n_a):
-                start(src, mine, a_send.at[i, d, da], a_recv.at[i, d, da], chip_peer[da - 1])
-            start(src, mine, c_send.at[i, d, 0], c_recv.at[i, d, 0], sibling)
-    for i in range(n_data):
-        for d in range(n_e):
-            eb = lax.rem(e + n_e - d, n_e)
-            for da in range(1, n_a):
-                other = block(i, eb, lax.rem(a + n_a - da, n_a), c)
-                remote(other, other, a_send.at[i, d, da], a_recv.at[i, d, da], sibling).wait_recv()
-                start(other, other, c_send.at[i, d, da], c_recv.at[i, d, da], sibling)
+                other = block(i, b, lax.rem(a + n_a - da, n_a), c)
+                landed(other, a_recv.at[i, b, da])
+                start(other, other, c_send.at[i, b, da], c_recv.at[i, b, da], sibling)
     for own in locals_:
         own.wait()
     for m in range(n_meta):
-        for d in range(1, n_e):
-            slot = outs[n_data + m].at[lax.rem(e + n_e - d, n_e)]
-            remote(slot, slot, m_send.at[m, d], m_recv.at[m, d], sibling).wait_recv()
+        for d in range(n_o):
+            landed(outs[n_data + m].at[source(n_o + d)], m_recv.at[m, n_o + d])
     for i in range(n_data):
-        for d in range(n_e):
-            eb = lax.rem(e + n_e - d, n_e)
+        for b in range(n_e):
             for da in range(n_a):
-                other = block(i, eb, lax.rem(a + n_a - da, n_a), 1 - c)
-                remote(other, other, c_send.at[i, d, da], c_recv.at[i, d, da], sibling).wait_recv()
+                landed(block(i, b, lax.rem(a + n_a - da, n_a), 1 - c), c_recv.at[i, b, da])
     for copy in sends:
         copy.wait_send()
 
@@ -132,35 +145,6 @@
     return [x.reshape(-1, x.shape[-1]) for x in outs]
 
 
-def core_kernel(x_ref, y_ref, send, recv):
-    e, a, c, _, n_a = place()
-    sibling = device(e, a, 1 - c)
-    greet([sibling])
-    share = y_ref.shape[2]
-    copies = []
-    for k in range(n_a):
-        start = pl.multiple_of((k * CORES + 1 - c) * share, share)
-        copy = remote(x_ref.at[:, pl.ds(start, share)], y_ref.at[k], send.at[k], recv.at[k], sibling)
-        copy.start()
-        copies.append(copy)
-    for copy in copies:
-        copy.wait()
-
-
-def core_swap(x, collective_id):
-    n_a = lax.axis_size("vocab") // CORES
-    share = x.shape[1] // (n_a * CORES)
-    dma = pltpu.SemaphoreType.DMA
-    return pl.pallas_call(
-        core_kernel,
-        out_shape=jax.ShapeDtypeStruct((n_a, x.shape[0], share), x.dtype),
-        in_specs=[VMEM],
-        out_specs=VMEM,
-        scratch_shapes=[dma((n_a,)), dma((n_a,))],
-        compiler_params=pltpu.CompilerParams(collective_id=collective_id, has_side_effects=True),
-    )(x)
-
-
 def swap_kernel(kind, n, x_ref, y_ref, send, recv):
     e, a, c, _, _ = place()
     me = {"expert": e, "chip": a, "vocab": a * CORES + c}[kind]
@@ -195,22 +179,99 @@
     )(x)
 
 
-def scatter_sum(partial, chip_type, expert_type, first_id):
+def scatter_kernel(x_ref, y_ref, from_core, to_chip, from_chip, own, to_row, from_row,
+                   core_send, core_recv, chip_send, chip_recv, row_send, row_recv):
     e, a, c, n_e, n_a = place()
-    rows, width = partial.shape
-    share = width // (n_a * CORES)
-    other = core_swap(partial, first_id)
-    by_chip = jnp.stack([
-        lax.dynamic_slice_in_dim(partial, (k * CORES + c) * share, share, 1) + other[k]
-        for k in range(n_a)
-    ])
-    arrived = swap(by_chip.astype(chip_type), "chip", n_a, first_id + 1)
-    total = lax.dynamic_index_in_dim(by_chip, a, 0, False)
-    total = total + jnp.sum(arrived.astype(jnp.float32), axis=0)
-    by_row = total.reshape(n_e, rows // n_e, share)
-    arrived = swap(by_row.astype(expert_type), "expert", n_e, first_id + 2)
-    own = lax.dynamic_index_in_dim(by_row, e, 0, False)
-    return own + jnp.sum(arrived.astype(jnp.float32), axis=0)
+    rows, share = y_ref.shape
+    sibling = device(e, a, 1 - c)
+    chip_at = [lax.rem(a + d, n_a) for d in range(n_a)]
+    row_at = [lax.rem(e + d, n_e) for d in range(n_e)]
+    greet([sibling] + [device(e, p, c) for p in chip_at[1:]]
+          + [device(p, a, c) for p in row_at[1:]])
+    order = list(range(1, n_e)) + [0]
+    sends = []
+
+    def piece(s, k, cb):
+        row = pl.multiple_of(row_at[s] * rows, rows)
+        column = pl.multiple_of((chip_at[k] * CORES + cb) * share, share)
+        return pl.ds(row, rows), pl.ds(column, share)
+
+    def core_copy(s, k):
+        return remote(x_ref.at[piece(s, k, 1 - c)], from_core.at[s, k], core_send.at[s, k],
+                      core_recv.at[s, k], sibling)
+
+    def chip_copy(s, k):
+        return remote(to_chip.at[s, k], from_chip.at[s, k], chip_send.at[s, k],
+                      chip_recv.at[s, k], device(e, chip_at[k], c))
+
+    def row_copy(s):
+        return remote(to_row.at[s], from_row.at[s], row_send.at[s], row_recv.at[s],
+                      device(row_at[s], a, c))
+
+    def start(copy):
+        copy.start()
+        sends.append(copy)
+
+    turns = list(range(1, n_a)) + [0]
+    for s in order:
+        for k in turns:
+            start(core_copy(s, k))
+
+    def first(s):
+        for k in turns:
+            core_copy(s, k).wait_recv()
+            term = x_ref[piece(s, k, c)] + from_core[s, k]
+            if k:
+                to_chip[s, k] = term.astype(to_chip.dtype)
+                start(chip_copy(s, k))
+            else:
+                own[s] = term
+
+    def second(s):
+        term = own[s]
+        for k in range(1, n_a):
+            chip_copy(s, k).wait_recv()
+            term = term + from_chip[s, k].astype(jnp.float32)
+        if s:
+            to_row[s] = term.astype(to_row.dtype)
+            start(row_copy(s))
+        else:
+            y_ref[...] = term
+
+    lag = 2
+    for step in range(n_e + lag):
+        if step < n_e:
+            first(order[step])
+        if step >= lag:
+            second(order[step - lag])
+    for s in range(1, n_e):
+        row_copy(s).wait_recv()
+        y_ref[...] += from_row[s].astype(jnp.float32)
+    for copy in sends:
+        copy.wait_send()
+
+
+def scatter_sum(partial, chip_type, row_type, collective_id):
+    n_e, n_a = lax.axis_size("expert"), lax.axis_size("vocab") // CORES
+    rows, share = partial.shape[0] // n_e, partial.shape[1] // (n_a * CORES)
+    dma = pltpu.SemaphoreType.DMA
+    return pl.pallas_call(
+        scatter_kernel,
+        out_shape=jax.ShapeDtypeStruct((rows, share), jnp.float32),
+        in_specs=[VMEM],
+        out_specs=VMEM,
+        scratch_shapes=[
+            pltpu.VMEM((n_e, n_a, rows, share), jnp.float32),
+            pltpu.VMEM((n_e, n_a, rows, share), chip_type),
+            pltpu.VMEM((n_e, n_a, rows, share), chip_type),
+            pltpu.VMEM((n_e, rows, share), jnp.float32),
+            pltpu.VMEM((n_e, rows, share), row_type),
+            pltpu.VMEM((n_e, rows, share), row_type),
+            dma((n_e, n_a)), dma((n_e, n_a)), dma((n_e, n_a)), dma((n_e, n_a)),
+            dma((n_e,)), dma((n_e,)),
+        ],
+        compiler_params=pltpu.CompilerParams(collective_id=collective_id, has_side_effects=True),
+    )(partial)
 
 
 def on_device(
@@ -275,7 +336,7 @@
     partial_grad = lax.dot_general(
         score_grad, head_weight, (((1,), (1,)), ((), ())), preferred_element_type=jnp.float32
     )
-    normed_grad = scatter_sum(partial_grad, jnp.bfloat16, jnp.bfloat16, 1)
+    normed_grad = scatter_sum(partial_grad, jnp.float32, jnp.bfloat16, 1)
     gained = gain_share * normed_grad
     mean_part = jnp.sum(unit_share * gained, axis=1, keepdims=True) / model_width
     mean_part = jnp.broadcast_to(mean_part, (rows_local, 128))
@@ -298,7 +359,7 @@
                 grad, weight, (((1,), (1,)), ((), ())), preferred_element_type=jnp.float32
             )
             partial_input = term if partial_input is None else partial_input + term
-    input_grad = scatter_sum(partial_input, jnp.float32, jnp.bfloat16, 6)
+    input_grad = scatter_sum(partial_input, jnp.float32, jnp.float32, 6)
     return (head_grad, residual_grad, input_grad)
 
 

time: 169 us -> 139 us (0.82)
  Pallas kernels: 112 us -> 95.1 us
  other arithmetic: 22.6 us -> 10.4 us
    pallas_call x5 -> x1, Pallas kernels: 53.8 us -> 5.12 us  [swap(): pl.pallas_call(functools.partial(swap_kernel, kind, n), out_shape=jax.Sha...]
    pallas_call x2, Pallas kernels: 10.7 us -> 45.7 us  [scatter_sum(): pl.pallas_call(scatter_kernel, out_shape=jax.ShapeDtypeStruct((rows, shar...]
    another operation x3 -> x0, other arithmetic: 4.51 us -> none  [scatter_sum(): jnp.stack([lax.dynamic_slice_in_dim(partial, (k * CORES + c) * share, sha...]
    pallas_call x2, Pallas kernels: 47.7 us -> 44.3 us  [gather_all(): pl.pallas_call(functools.partial(gather_kernel, n_data, n_meta), out_shap...]
    add x3 -> x0, other arithmetic: 2.95 us -> none  [the longest x2 2.3 us: scatter_sum(): total = total + jnp.sum(arrived.astype(jnp.float32), axis=0)]
    convert_element_type x3 -> x0, other arithmetic: 2.33 us -> none  [the longest x2 1.47 us: scatter_sum(): arrived = swap(by_row.astype(expert_type), 'expert', n_e, first_id + 2)]
    reduce_sum x2 -> x0, other arithmetic: 1.96 us -> none  [scatter_sum(): return own + jnp.sum(arrived.astype(jnp.float32), axis=0)]
where the time goes in v2:
time: 139 us
  Pallas kernels  95.1 us (68%)
  matrix products  28 us (20%)
  other arithmetic  10.4 us (7%)
  local copies, waits for them, and re-layouts  4.26 us (3%)
    pallas_call x2, Pallas kernels, scatter_sum(): pl.pallas_call(scatter_kernel, out_shape=jax.ShapeDtypeStruct((rows, shar...  45.7 us
    pallas_call x2, Pallas kernels, gather_all(): pl.pallas_call(functools.partial(gather_kernel, n_data, n_meta), out_shap...  44.3 us
    dot_general x4, matrix products, on_device(): lax.dot_general(grad, weight, (((1,), (1,)), ((), ())), preferred_element...  16.4 us
    pallas_call x1, Pallas kernels, swap(): pl.pallas_call(functools.partial(swap_kernel, kind, n), out_shape=jax.Sha...  5.12 us
    dot_general x2, matrix products, on_device(): lax.dot_general(residual_all, w_down[i], (((1,), (1,)), ((), ())), prefer...  4.34 us

profile of v2, /device:TPU:0, one launch (start us, length us, event | category | flops | bytes accessed | tf_op | source)
XLA Modules:
  0.0 138.5 jit_solution(6203691536811123030)
XLA Ops:
  0.6 0.0 copy-start
  0.7 0.9 dynamic_slice.13
  1.5 1.0 multiply_reduce_fusion
  2.6 1.5 %multiply_convert_fusion.4.refs_0_ = bf16[32,512]{1,0:T(8,128)(2,1)} fusion(f32[512]{0:T(512)S(1)} %dynamic_slice.13, f32[32]{0:T(128)S(1)} %add_sqrt_fusion, bf16[32,2048]{1,0:T(8,128)(2,1)} %param.12, s32[]{:T(128)S(6)} %select_n.16), kind=kLoop, calls=%fused_computation.60 | loop fusion | flops 65536 | bytes 67716 | tf_op jit(solution)/shard_map/convert_element_type | solution.py:308
  4.0 1.4 constant_dynamic-slice_fusion.2.refs_1_
  5.4 0.7 select_reduce_fusion
  6.1 0.1 copy.26
  6.2 0.8 select_reduce_fusion.1
  7.0 0.1 copy.27
  7.1 0.7 convert_bitcast_fusion
  7.7 0.1 copy.28
  7.8 0.7 select_maximum_fusion.refs_2_
  8.5 27.3 %shard_map.139 = (bf16[8,32,2048]{2,1,0:T(8,128)(2,1)}, bf16[8,32,2048]{2,1,0:T(8,128)(2,1)}, f32[8,32,128]{2,1,0:T(8,128)}) custom-call(bf16[32,512]{1,0:T(8,128)(2,1)} %multiply_convert_fusion.4.refs_0_, bf16[32,512]{1,0:T(8,128)(2,1)} %constant_dynamic-slice_fusion.2.refs_1_, f32[32,128]{1,0:T(8,128)} %select_maximum_fusion.refs_2_), custom_call_target="tpu_custom_call" | custom-call | tf_op jit(solution)/shard_map/pallas_call | solution.py:131
  35.8 1.3 constant_dynamic-slice_fusion.1
  37.1 0.1 copy.37
  37.2 0.1 copy.33
  37.3 0.0 copy-done
  37.3 2.0 %fusion.2 = bf16[256,384]{1,0:T(8,128)(2,1)S(1)} fusion(bf16[256,2048]{1,0:T(8,128)(2,1)} %bitcast.55, bf16[2048,384]{1,0:T(8,128)(2,1)S(1)} %copy-done, f32[256]{0:T(256)S(1)} %bitcast.61, s32[384]{0:T(512)S(1)} %iota_add_fusion, s32[256]{0:T(256)S(1)} %bitcast.60), kind=kOutput, calls=%fused_computation.6 | convolution fusion | flops 403144704 | bytes 2821632 | tf_op jit(solution)/shard_map/dot_general | solution.py:329
  39.2 0.0 copy-start.5
  39.2 2.1 %fusion.53.x_ref = f32[256,2048]{1,0:T(8,128)} fusion(bf16[256,384]{1,0:T(8,128)(2,1)S(1)} %fusion.2, bf16[2048,384]{1,0:T(8,128)(2,1)S(1)} %copy-done), kind=kOutput, calls=%fused_computation.82 | convolution fusion | flops 402653184 | bytes 3866624 | tf_op jit(solution)/shard_map/dot_general | solution.py:336
  41.3 22.4 %shard_map.140 = f32[32,512]{1,0:T(8,128)} custom-call(f32[256,2048]{1,0:T(8,128)} %fusion.53.x_ref), custom_call_target="tpu_custom_call" | custom-call | tf_op jit(solution)/shard_map/pallas_call | solution.py:258
  63.7 0.0 copy-done.5
  63.7 1.0 multiply_reduce_fusion.1
  64.7 0.7 broadcast_in_dim.48.x_ref
  65.4 5.1 %shard_map.141 = f32[3,32,128]{2,1,0:T(8,128)} custom-call(f32[32,128]{1,0:T(8,128)} %broadcast_in_dim.48.x_ref), custom_call_target="tpu_custom_call" | custom-call | tf_op jit(solution)/shard_map/pallas_call | solution.py:172
  70.5 0.8 reduce_sum.49
  71.4 0.2 fusion.46
  71.5 1.7 %fusion.51 = (bf16[32,512]{1,0:T(8,128)(2,1)}, f32[32,512]{1,0:T(8,128)}) fusion(f32[32]{0:T(128)S(1)} %fusion.46, f32[32]{0:T(128)S(1)} %add_sqrt_fusion, bf16[32,2048]{1,0:T(8,128)(2,1)S(1)} %copy-done.5, s32[]{:T(128)S(6)} %select_n.16, f32[32,512]{1,0:T(8,128)} %shard_map.140, f32[512]{0:T(512)S(1)} %dynamic_slice.13), kind=kLoop, calls=%fused_computation.80 | loop fusion | flops 114688 | bytes 198916 | tf_op jit(solution)/shard_map/convert_element_type | solution.py:345
  73.2 17.0 %shard_map.142 = bf16[8,32,2048]{2,1,0:T(8,128)(2,1)} custom-call(bf16[32,512]{1,0:T(8,128)(2,1)} %get-tuple-element.9.refs_0_), custom_call_target="tpu_custom_call" | custom-call | tf_op jit(solution)/shard_map/pallas_call | solution.py:131
  90.2 0.1 copy.35
  90.3 2.2 %convolution_multiply_fusion.3 = f32[256,256]{1,0:T(8,128)S(1)} fusion(bf16[256,2048]{1,0:T(8,128)(2,1)} %bitcast.58, bf16[2,256,2048]{2,1,0:T(8,128)(2,1)} %param.23, f32[256]{0:T(256)S(1)} %bitcast.63), kind=kOutput, calls=%fused_computation.14 | convolution fusion | flops 268500992 | bytes 2360320 | tf_op jit(solution)/shard_map/dot_general | solution.py:351
  92.5 0.0 copy-done.1
  92.5 0.0 copy-done.3
  92.5 0.4 fusion.18
  93.0 4.1 %fusion.9 = f32[256,2048]{1,0:T(8,128)} fusion(f32[256,256]{1,0:T(8,128)S(1)} %convolution_multiply_fusion.3, bf16[256,2048]{1,0:T(8,128)(2,1)S(1)} %bitcast.52, bf16[2,2048,256]{2,1,0:T(8,128)(2,1)} %param.21, bf16[2,2048,256]{2,1,0:T(8,128)(2,1)} %param.22, f32[256,256]{1,0:T(8,128)S(1)} %fusion.18), kind=kOutput, calls=%fused_computation.17 | convolution fusion | flops 537526272 | bytes 5767168 | tf_op jit(solution)/shard_map/dot_general | solution.py:358
  97.1 3.7 %convolution_add_fusion.2 = f32[256,2048]{1,0:T(8,128)} fusion(f32[256,2048]{1,0:T(8,128)} %fusion.9, bf16[2,2048,256]{2,1,0:T(8,128)(2,1)} %param.22, f32[256,256]{1,0:T(8,128)S(1)} %convolution_multiply_fusion.3, f32[256,256]{1,0:T(8,128)S(1)} %fusion.18), kind=kOutput, calls=%fused_computation.2 | convolution fusion | flops 269352960 | bytes 5767168 | tf_op jit(solution)/shard_map/dot_general | solution.py:358
  100.8 0.1 copy.36
  100.9 2.2 %convolution_multiply_fusion.1 = f32[256,256]{1,0:T(8,128)S(1)} fusion(bf16[256,2048]{1,0:T(8,128)(2,1)} %bitcast.59, bf16[2,256,2048]{2,1,0:T(8,128)(2,1)} %param.23, f32[256]{0:T(256)S(1)} %bitcast.62), kind=kOutput, calls=%fused_computation.10 | convolution fusion | flops 268500992 | bytes 2360320 | tf_op jit(solution)/shard_map/dot_general | solution.py:351
  103.1 0.1 copy-done.4
  103.1 0.4 fusion.11
  103.6 4.8 %convolution_add_fusion.1 = f32[256,2048]{1,0:T(8,128)} fusion(f32[256,2048]{1,0:T(8,128)} %convolution_add_fusion.2, f32[256,256]{1,0:T(8,128)S(1)} %convolution_multiply_fusion.1, bf16[256,2048]{1,0:T(8,128)(2,1)S(1)} %bitcast.54, bf16[2,2048,256]{2,1,0:T(8,128)(2,1)} %param.21, bf16[2,2048,256]{2,1,0:T(8,128)(2,1)} %param.22, f32[256,256]{1,0:T(8,128)S(1)} %fusion.11), kind=kOutput, calls=%fused_computation.1 | convolution fusion | flops 538050560 | bytes 7864320 | tf_op jit(solution)/shard_map/dot_general | solution.py:358
  108.4 3.7 %convolution_add_fusion.x_ref = f32[256,2048]{1,0:T(8,128)} fusion(f32[256,2048]{1,0:T(8,128)} %convolution_add_fusion.1, bf16[2,2048,256]{2,1,0:T(8,128)(2,1)} %param.22, f32[256,256]{1,0:T(8,128)S(1)} %convolution_multiply_fusion.1, f32[256,256]{1,0:T(8,128)S(1)} %fusion.11), kind=kOutput, calls=%fused_computation | convolution fusion | flops 269352960 | bytes 5767168 | tf_op jit(solution)/shard_map/dot_general | solution.py:358
  112.1 23.3 %shard_map.143 = f32[32,512]{1,0:T(8,128)} custom-call(f32[256,2048]{1,0:T(8,128)} %convolution_add_fusion.x_ref), custom_call_target="tpu_custom_call" | custom-call | tf_op jit(solution)/shard_map/pallas_call | solution.py:258
  135.5 0.0 copy-done.2
  135.5 0.0 copy-start.6
  135.5 2.4 %fusion.52 = f32[2048,384]{1,0:T(8,128)} fusion(bf16[256,2048]{1,0:T(8,128)(2,1)S(1)} %bitcast.56, bf16[256,384]{1,0:T(8,128)(2,1)S(1)} %fusion.2), kind=kOutput, calls=%fused_computation.81 | convolution fusion | flops 402653184 | bytes 4390912 | tf_op jit(solution)/shard_map/dot_general | solution.py:333
  137.9 0.0 copy-done.6
  137.9 0.6 copy.39
  (7 shorter events, 0.0 us)
Async XLA Ops:
  0.6 36.6 %copy-start = (bf16[2048,384]{1,0:T(8,128)(2,1)S(1)}, bf16[2048,384]{1,0:T(8,128)(2,1)}, u32[]{:S(2)}) copy-start(bf16[2048,384]{1,0:T(8,128)(2,1)} %param.15) | copy-start | bytes 4718596
  39.2 24.4 %copy-start.5 = (bf16[32,2048]{1,0:T(8,128)(2,1)S(1)}, bf16[32,2048]{1,0:T(8,128)(2,1)}, u32[]{:S(2)}) copy-start(bf16[32,2048]{1,0:T(8,128)(2,1)} %param.12) | copy-start | bytes 393220
  71.4 21.1 %copy-start.1 = (bf16[8,32,2048]{2,1,0:T(8,128)(2,1)S(1)}, bf16[8,32,2048]{2,1,0:T(8,128)(2,1)}, u32[]{:S(2)}) copy-start(bf16[8,32,2048]{2,1,0:T(8,128)(2,1)} %get-tuple-element.8) | copy-start | bytes 3145732
  90.3 2.2 %copy-start.3 = (bf16[2,2048,256]{2,1,0:T(8,128)(2,1)S(1)}, bf16[2,2048,256]{2,1,0:T(8,128)(2,1)}, u32[]{:S(2)}) copy-start(bf16[2,2048,256]{2,1,0:T(8,128)(2,1)} %param.21) | copy-start | bytes 6291460
  100.9 2.2 %copy-start.4 = (bf16[2,2048,256]{2,1,0:T(8,128)(2,1)S(1)}, bf16[2,2048,256]{2,1,0:T(8,128)(2,1)}, u32[]{:S(2)}) copy-start(bf16[2,2048,256]{2,1,0:T(8,128)(2,1)} %param.21) | copy-start | bytes 6291460
  112.1 23.3 %copy-start.2 = (bf16[8,32,2048]{2,1,0:T(8,128)(2,1)S(1)}, bf16[8,32,2048]{2,1,0:T(8,128)(2,1)}, u32[]{:S(2)}) copy-start(bf16[8,32,2048]{2,1,0:T(8,128)(2,1)} %get-tuple-element.6) | copy-start | bytes 3145732
  135.5 2.4 %copy-start.6 = (f32[32,512]{1,0:T(8,128)S(1)}, f32[32,512]{1,0:T(8,128)}, u32[]{:S(2)}) copy-start(f32[32,512]{1,0:T(8,128)} %shard_map.143) | copy-start | bytes 196612
